TPU v7x, 32 devices: a whole 2x2x4 slice. The times are simulated.
32 devices in a mesh: band: 2 (over x), tm: 16 (over z, y, core).
Axes of the slice: x: 2, y: 2, z: 4, core: 2. Of those that a mesh axis runs over, the one named last changes fastest.
Arguments:
- volts: int32 [8, 2, 3145728], P('band', None, 'tm'), parts along dimension 0, may hold values from -128 to 127, as said below
- taps: float32 [16, 4096], replicated, may hold values from -0.024 to 0.024
- pairs: int32 [4, 2], replicated, may hold values from 0 to 3, as said below
Outputs:
- coherence: float32 [8, 4096], P('band'), parts along dimension 0
- normalized: float32 [2, 8, 768, 4096], P(None, 'band', 'tm'), parts along dimension 1
There are 2 independent parts, one for each index of `band`. A program takes and returns all parts, laid end to end along the dimension named above; an argument that names none is the same for every part. Nothing has to cross between parts.
Inputs may be any that keep to these rules, and one draw needn't show every extreme that they name: `volts`: every sample is a whole number of the int8 range. Each pair names a stream of the first antenna (0 or 1) and then one of the second antenna (2 or 3); the four pairs are distinct.
All inputs are finite; a program needn't handle non-finite values.
Results may differ from a plain program's by a relative error of at most 0.000067.
Values sent between devices are 32-bit elements; how exact they have to be, the bound alone decides.
A program may use at most 128 MiB of HBM per device.

v0:
```python
import functools
import math

import jax
import jax.numpy as jnp
import numpy as np
from jax import lax
from jax.experimental import pallas as pl
from jax.experimental.pallas import tpu as pltpu
from jax.sharding import PartitionSpec as P

LANES = 128
SUB = 8


def matrices(channels):
    radix = channels // LANES
    lane = np.arange(LANES)
    a = (LANES // radix) * (lane % radix) + lane // radix
    angle = 2.0 * np.pi * ((a[:, None] * lane[None, :]) % LANES) / LANES
    c, s = np.cos(angle), np.sin(angle)
    full = np.block([[c, -s], [s, c]]) / math.sqrt(channels)
    high = full.astype(jnp.bfloat16)
    low = (full - high.astype(np.float64)).astype(jnp.bfloat16)
    return jnp.asarray(high), jnp.asarray(low)


def twiddles(channels):
    radix = channels // LANES
    b = np.arange(radix)
    k = np.arange(LANES)
    angle = 2.0 * np.pi * ((b[:, None] * k[None, :]) % channels) / channels
    both = np.stack([np.cos(angle), np.sin(angle)]).astype(np.float32)
    return jnp.asarray(np.broadcast_to(both[:, :, None], (2, radix, SUB, LANES)))


def turn(z, num, den):
    re, im = z
    num = num % den
    if num == 0:
        return z
    if 4 * num == den:
        return (im, -re)
    if 2 * num == den:
        return (-re, -im)
    if 4 * num == 3 * den:
        return (-im, re)
    h = np.float32(math.sqrt(0.5))
    if 8 * num == den:
        return ((re + im) * h, (im - re) * h)
    if 8 * num == 3 * den:
        return ((im - re) * h, -((re + im) * h))
    c = np.float32(math.cos(2.0 * math.pi * num / den))
    s = np.float32(math.sin(2.0 * math.pi * num / den))
    return (re * c + im * s, im * c - re * s)


def add(x, y):
    return (x[0] + y[0], x[1] + y[1])


def sub(x, y):
    return (x[0] - y[0], x[1] - y[1])


def dft(items):
    n = len(items)
    if n == 1:
        return items
    if n == 2:
        return [add(*items), sub(*items)]
    if n == 4:
        p, q = add(items[0], items[2]), sub(items[0], items[2])
        r, s = add(items[1], items[3]), sub(items[1], items[3])
        down = (q[0] + s[1], q[1] - s[0])
        up = (q[0] - s[1], q[1] + s[0])
        return [add(p, r), down, sub(p, r), up]
    if n == 8:
        even, odd = dft(items[0::2]), dft(items[1::2])
        odd = [turn(z, i, 8) for i, z in enumerate(odd)]
        return [add(e, o) for e, o in zip(even, odd)] + [sub(e, o) for e, o in zip(even, odd)]
    inner = n // 4
    groups = [[turn(z, g * i, n) for i, z in enumerate(dft(items[g::4]))] for g in range(4)]
    out = [None] * n
    for i in range(inner):
        for j, z in enumerate(dft([groups[g][i] for g in range(4)])):
            out[i + inner * j] = z
    return out


def swap_lanes(rows):
    rows = list(rows)
    lane = lax.broadcasted_iota(jnp.int32, (SUB, LANES), 1)
    step = 1
    while step < len(rows):
        low = (lane & step) == 0
        for i in range(len(rows)):
            if i & step == 0:
                a, b = rows[i], rows[i + step]
                rows[i] = jnp.where(low, a, pltpu.roll(b, step, 1))
                rows[i + step] = jnp.where(low, pltpu.roll(a, LANES - step, 1), b)
        step *= 2
    return rows


def block_work(load, pairs, taps, high, low, twist, out, acc, filt, left_hi, left_lo, mid, spec):
    streams = spec.shape[0]
    ntaps, rows_frame = taps.shape[0], taps.shape[1]
    radix = rows_frame // 2

    @pl.loop(0, streams)
    def _(s):
        @pl.loop(0, rows_frame // SUB)
        def _(c):
            rows = pl.ds(pl.multiple_of(c * SUB, SUB), SUB)
            tap = [taps[t, rows, :] for t in range(ntaps)]
            x = [load(s, i, rows).astype(jnp.float32) for i in range(SUB + ntaps - 1)]
            for f in range(SUB):
                total = tap[0] * x[f + ntaps - 1]
                for t in range(1, ntaps):
                    total = total + tap[t] * x[f + ntaps - 1 - t]
                at = pl.multiple_of(f * rows_frame + c * SUB, SUB)
                filt[s, pl.ds(at, SUB), :] = total

        for comp in range(2):
            rows = [filt[s, pl.ds(2 * r + comp, SUB, stride=rows_frame), :] for r in range(radix)]
            rows = swap_lanes(rows)
            for b in range(0, radix, 2):
                both = jnp.concatenate([rows[b], rows[b + 1]], axis=0)
                hi = both.astype(jnp.bfloat16)
                lo = (both - hi.astype(jnp.float32)).astype(jnp.bfloat16)
                at = pl.multiple_of(s * radix * SUB + b * SUB, 2 * SUB)
                where = (pl.ds(at, 2 * SUB), pl.ds(comp * LANES, LANES))
                left_hi[where] = hi
                left_lo[where] = lo

    dot = functools.partial(jnp.dot, preferred_element_type=jnp.float32)

    @pl.loop(0, streams)
    def _(s):
        at = pl.ds(pl.multiple_of(s * radix * SUB, radix * SUB), radix * SUB)
        hi, lo = left_hi[at, :], left_lo[at, :]
        mid[at, :] = dot(hi, high[...]) + (dot(lo, high[...]) + dot(hi, low[...]))

    @pl.loop(0, streams)
    def _(s):
        items = []
        for b in range(radix):
            at = pl.ds(pl.multiple_of(s * radix * SUB + b * SUB, SUB), SUB)
            re, im = mid[at, 0:LANES], mid[at, LANES : 2 * LANES]
            if b:
                c, n = twist[0, b], twist[1, b]
                re, im = re * c + im * n, im * c - re * n
            items.append((re, im))
        for k, z in enumerate(dft(items)):
            spec[s, 0, k] = z[0]
            spec[s, 1, k] = z[1]

    npairs = pairs.shape[0]

    @pl.loop(0, radix)
    def _(k):
        cols = pl.ds(pl.multiple_of(k * LANES, LANES), LANES)
        for s in range(streams):
            re, im = spec[s, 0, k], spec[s, 1, k]
            acc[s, :, cols] += re * re + im * im
        for p in range(npairs):
            a, b = pairs[p, 0], pairs[p, 1]
            lr, li, rr, ri = spec[a, 0, k], spec[a, 1, k], spec[b, 0, k], spec[b, 1, k]
            pr = lr * rr + li * ri
            pi = li * rr - lr * ri
            out[0, p, :, cols] = pr
            out[1, p, :, cols] = pi
            acc[streams + p, :, cols] += pr
            acc[streams + npairs + p, :, cols] += pi


def finish(acc, sums):
    for i in range(acc.shape[0]):
        sums[i : i + 1, :] = jnp.sum(acc[i], axis=0, keepdims=True)


def inner_kernel(pairs, pp, p, c, taps, high, low, twist, out, sums, acc, *scratch):
    j = pl.program_id(0)

    @pl.when(j == 0)
    def _():
        acc[...] = jnp.zeros_like(acc)

    def load(s, i, rows):
        if i < 7:
            return pp[s, i + 1, rows, :]
        if i < 15:
            return p[s, i - 7, rows, :]
        return c[s, i - 15, rows, :]

    block_work(load, pairs, taps, high, low, twist, out, acc, *scratch)

    @pl.when(j == pl.num_programs(0) - 1)
    def _():
        finish(acc, sums)


def edge_kernel(pairs, halo, c0, c, taps, high, low, twist, _, out, sums, acc, *scratch):
    j = pl.program_id(0)

    @pl.when(j == 0)
    def _():
        acc[...] = jnp.zeros_like(acc)

    def load(s, i, rows):
        if i < 7:
            return halo[s, i + j * SUB, rows, :]
        if i < 15:
            return jnp.where(j == 0, halo[s, i, rows, :], c0[s, i - 7, rows, :])
        return c[s, i - 15, rows, :]

    block_work(load, pairs, taps, high, low, twist, out, acc, *scratch)

    @pl.when(j == pl.num_programs(0) - 1)
    def _():
        finish(acc, sums)


def scale_kernel(frames_all, pairs, sums, prod, coherence, out):
    npairs = pairs.shape[0]
    streams = sums.shape[0] - 2 * npairs
    for p in range(npairs):
        a, b = pairs[p, 0], pairs[p, 1]
        mean_a = sums[pl.ds(a, 1), :] / frames_all
        mean_b = sums[pl.ds(b, 1), :] / frames_all
        re = sums[streams + p : streams + p + 1, :] / frames_all
        im = sums[streams + npairs + p : streams + npairs + p + 1, :] / frames_all
        denom = (mean_a + 1e-06) * (mean_b + 1e-06)

        @pl.when(pl.program_id(0) == 0)
        def _():
            coherence[p : p + 1, :] = (re * re + im * im) / denom

        factor = 1.0 / jnp.sqrt(denom)
        out[0, p] = prod[0, p] * factor
        out[1, p] = prod[1, p] * factor


def on_device(volts, taps, pairs):
    streams, comps, local = volts.shape
    ntaps, channels = taps.shape
    radix = channels // LANES
    edge = ntaps - 1
    frames = local // channels
    rows_frame = radix * comps
    blocks = frames // SUB
    npairs = pairs.shape[0]
    nsums = streams + 2 * npairs
    view = volts.reshape(streams, comps, frames * radix, LANES).transpose(0, 2, 1, 3)
    view = view.reshape(streams, frames, rows_frame, LANES)
    size = lax.axis_size("tm")
    halo = lax.ppermute(view[:, frames - edge :], "tm", [(i, i + 1) for i in range(size - 1)])
    taps2 = jnp.repeat(taps.reshape(ntaps, radix, LANES), comps, axis=1)
    high, low = matrices(channels)
    twist = twiddles(channels)

    rows = streams * radix * SUB
    scratch = [
        pltpu.VMEM((nsums, SUB, channels), jnp.float32),
        pltpu.VMEM((streams, SUB * rows_frame, LANES), jnp.float32),
        pltpu.VMEM((rows, 2 * LANES), jnp.bfloat16),
        pltpu.VMEM((rows, 2 * LANES), jnp.bfloat16),
        pltpu.VMEM((rows, 2 * LANES), jnp.float32),
        pltpu.VMEM((streams, comps, radix, SUB, LANES), jnp.float32),
    ]
    smem = pl.BlockSpec(memory_space=pltpu.SMEM)

    def whole(*dims):
        return pl.BlockSpec(dims, lambda j: (0,) * len(dims))

    tables = [
        whole(ntaps, rows_frame, LANES),
        whole(2 * LANES, 2 * LANES),
        whole(2 * LANES, 2 * LANES),
        whole(2, radix, SUB, LANES),
    ]
    frame_dims = (streams, SUB, rows_frame, LANES)
    prod_dims = (2, npairs, SUB, channels)
    prod_type = jax.ShapeDtypeStruct((2, npairs, frames, channels), jnp.float32)
    sums_type = jax.ShapeDtypeStruct((nsums, channels), jnp.float32)
    first = 2

    def params():
        return pltpu.CompilerParams(vmem_limit_bytes=48 * 1024 * 1024)

    def cost(n):
        return pl.CostEstimate(flops=n * 500_000_000, bytes_accessed=n * 4_000_000, transcendentals=0)

    prod, sums_inner = pl.pallas_call(
        inner_kernel,
        grid=(blocks - first,),
        in_specs=[smem]
        + [pl.BlockSpec(frame_dims, functools.partial(lambda d, j: (0, j + d, 0, 0), d)) for d in range(3)]
        + tables,
        out_specs=[
            pl.BlockSpec(prod_dims, lambda j: (0, 0, j + first, 0)),
            whole(nsums, channels),
        ],
        out_shape=[prod_type, sums_type],
        scratch_shapes=scratch,
        compiler_params=params(),
        cost_estimate=cost(blocks - first),
        name="inner",
    )(pairs, view, view, view, taps2, high, low, twist)

    prod, sums_edge = pl.pallas_call(
        edge_kernel,
        grid=(first,),
        in_specs=[smem, whole(streams, edge, rows_frame, LANES), whole(*frame_dims)]
        + [pl.BlockSpec(frame_dims, lambda j: (0, j, 0, 0))]
        + tables
        + [pl.BlockSpec(memory_space=pl.ANY)],
        out_specs=[
            pl.BlockSpec(prod_dims, lambda j: (0, 0, j, 0)),
            whole(nsums, channels),
        ],
        out_shape=[prod_type, sums_type],
        scratch_shapes=scratch,
        input_output_aliases={8: 0},
        compiler_params=params(),
        cost_estimate=cost(first),
        name="edge",
    )(pairs, halo, view, view, taps2, high, low, twist, prod)

    sums = lax.psum(sums_inner + sums_edge, "tm")
    coherence, normalized = pl.pallas_call(
        functools.partial(scale_kernel, frames * size),
        grid=(blocks,),
        in_specs=[smem, whole(nsums, channels), pl.BlockSpec(prod_dims, lambda j: (0, 0, j, 0))],
        out_specs=[whole(npairs, channels), pl.BlockSpec(prod_dims, lambda j: (0, 0, j, 0))],
        out_shape=[jax.ShapeDtypeStruct((npairs, channels), jnp.float32), prod_type],
        compiler_params=params(),
        name="scale",
    )(pairs, sums, prod)
    return (coherence, normalized)


def solution(mesh):
    return jax.shard_map(
        on_device,
        mesh=mesh,
        in_specs=(P("band", None, "tm"), P(), P()),
        out_specs=(P("band", None), P(None, "band", "tm", None)),
        check_vma=False,
    )
```

profile of v0, /device:TPU:0, one launch (start us, length us, event | category | flops | bytes accessed | tf_op | source)
XLA Modules:
  0.0 170.1 jit_solution(4055123414357427622)
XLA Ops:
  7.2 0.0 all-reduce.2.cloned.1.call-start
  7.2 3.1 %slice.4 = s32[4,15,64,128]{3,2,1,0:T(8,128)} slice(s32[4,48,64,128]{3,2,1,0:T(8,128)} %bitcast.10), slice={[0:4], [33:48], [0:64], [0:128]} | slice | bytes 3932160 | tf_op jit(solution)/shard_map/slice | solution.py:258
  10.3 2.5 %collective-permute-start = (s32[4,15,64,128]{3,2,1,0:T(8,128)}, s32[4,15,64,128]{3,2,1,0:T(8,128)S(1)}, u32[]{:S(2)}, u32[]{:S(2)}) collective-permute-start(s32[4,15,64,128]{3,2,1,0:T(8,128)} %slice.4), channel_id=1, source_target_pairs={{0,1},{1,2},{2,3},{3,4},{4,5},{5,6},{6,7},{7,8},{8,9},{9,10},{10,1... | collective-permute-start | bytes 5898248 | tf_op jit(solution)/shard_map/ppermute | solution.py:258
  12.8 0.8 copy.12.pairs
  13.5 1.0 copy.13
  14.5 0.2 broadcast_in_dim.3
  14.7 0.8 jit_solution_.3.twist
  15.5 0.0 copy-start
  15.5 0.9 copy-done
  16.4 0.0 copy-start.1
  16.4 0.9 copy-done.1
  17.3 28.6 %inner.1 = (f32[2,4,48,4096]{3,2,1,0:T(8,128)}, f32[12,4096]{1,0:T(8,128)S(1)}) custom-call(s32[4,2]{1,0:T(4,128)S(1)} %copy.12.pairs, s32[4,48,64,128]{3,2,1,0:T(8,128)} %bitcast.11, s32[4,48,64,128]{3,2,1,0:T(8,128)} %bitcast.12, s32[4,48,64,128]{3,2,1,0:T(8,128)} %bitcast.13, f32[16,64,128]{2,1,0:T(8,128)S(1)} %bitcast.8, bf16[256,256]{1,0:T(8,128)(2,1)S(1)} %copy-done.1, ...), custom_call_target="tpu_custom_call" | custom-call | flops 2000000000 | bytes 16000000 | tf_op jit(solution)/shard_map/inner/pallas_call | solution.py:295
  45.9 0.0 collective-permute-done.halo
  45.9 16.0 %edge.1 = (f32[2,4,48,4096]{3,2,1,0:T(8,128)}, f32[12,4096]{1,0:T(8,128)S(1)}) custom-call(s32[4,2]{1,0:T(4,128)S(1)} %copy.12.pairs, s32[4,15,64,128]{3,2,1,0:T(8,128)S(1)} %collective-permute-done.halo, s32[4,48,64,128]{3,2,1,0:T(8,128)} %bitcast.14, s32[4,48,64,128]{3,2,1,0:T(8,128)} %bitcast.15, ...), custom_call_target="tpu_custom_call", output_to_operand_aliasing={{0}: (8, {})} | custom-call | flops 1000000000 | bytes 8000000 | tf_op jit(solution)/shard_map/edge/pallas_call | solution.py:312
  62.0 0.7 add.5
  62.7 0.0 all-reduce.2.cloned.1.call-update
  62.7 92.3 %all-reduce.2.cloned.1.call-done.sums = f32[12,4096]{1,0:T(8,128)} async-done(((f32[12,4096]{1,0:T(8,128)}), f32[12,4096]{1,0:T(8,128)}) %all-reduce.2.cloned.1.call-update) | async-done | bytes 196624 | tf_op jit(solution)/shard_map/psum | solution.py:331
  155.0 0.0 copy-start.2
  155.0 0.9 copy-done.2
  156.0 7.2 %scale.1 = (f32[4,4096]{1,0:T(4,128)}, f32[2,4,48,4096]{3,2,1,0:T(8,128)}) custom-call(s32[4,2]{1,0:T(4,128)S(1)} %copy.12.pairs, f32[12,4096]{1,0:T(8,128)S(1)} %copy-done.2, f32[2,4,48,4096]{3,2,1,0:T(8,128)} %get-tuple-element.9.prod), custom_call_target="tpu_custom_call" | custom-call | tf_op jit(solution)/shard_map/scale/pallas_call | solution.py:332
Async XLA Ops:
  7.2 147.9 %all-reduce.2.cloned.1.call-start = ((), (), s32[]{:S(2)}) async-start(), calls=%async_computation | async-start | bytes 524288 | tf_op jit(solution)/shard_map/psum | solution.py:331
  10.3 35.7 %collective-permute-start = (s32[4,15,64,128]{3,2,1,0:T(8,128)}, s32[4,15,64,128]{3,2,1,0:T(8,128)S(1)}, u32[]{:S(2)}, u32[]{:S(2)}) collective-permute-start(s32[4,15,64,128]{3,2,1,0:T(8,128)} %slice.4), channel_id=1, source_target_pairs={{0,1},{1,2},{2,3},{3,4},{4,5},{5,6},{6,7},{7,8},{8,9},{9,10},{10,1... | collective-permute-start | bytes 5898248 | tf_op jit(solution)/shard_map/ppermute | solution.py:258
  15.5 0.9 copy-start
  16.4 0.9 copy-start.1
  155.0 0.9 copy-start.2
Sparse Core Ops, SparseCore 0:
  62.8 92.1 all-reduce.1
where the time goes:
time: 171 us; the launch traced here: 170 us
  waiting for transfers between devices  92.4 us (54%)
  Pallas kernels  51.8 us (30%)
  between operations  14.1 us (8%)
  local copies, waits for them, and re-layouts  8.54 us (5%)
  starting transfers between devices  2.55 us (1%)
    psum x1, waiting for transfers between devices, on_device(): sums = lax.psum(sums_inner + sums_edge, 'tm')  92.3 us
    pallas_call x1, Pallas kernels, on_device(): pl.pallas_call(inner_kernel, grid=(blocks - first,), in_specs=[smem] + [p...  28.6 us
    pallas_call x1, Pallas kernels, on_device(): pl.pallas_call(edge_kernel, grid=(first,), in_specs=[smem, whole(streams,...  16 us
    pallas_call x1, Pallas kernels, on_device(): pl.pallas_call(functools.partial(scale_kernel, frames * size), grid=(bloc...  7.21 us
    unnamed x8, local copies, waits for them, and re-layouts  4.52 us
  transfers between devices with their start and end apart: 2, of which 1 were waited for; matrix products, arithmetic and copies ran while one was open for 2% of the time, Pallas kernels for 17%

commit v1 on v0

--- a/solution.py
+++ b/solution.py
@@ -22,7 +22,7 @@
     full = np.block([[c, -s], [s, c]]) / math.sqrt(channels)
     high = full.astype(jnp.bfloat16)
     low = (full - high.astype(np.float64)).astype(jnp.bfloat16)
-    return jnp.asarray(high), jnp.asarray(low)
+    return jnp.asarray(np.stack([high, low]))
 
 
 def twiddles(channels):
@@ -31,7 +31,7 @@
     k = np.arange(LANES)
     angle = 2.0 * np.pi * ((b[:, None] * k[None, :]) % channels) / channels
     both = np.stack([np.cos(angle), np.sin(angle)]).astype(np.float32)
-    return jnp.asarray(np.broadcast_to(both[:, :, None], (2, radix, SUB, LANES)))
+    return jnp.asarray(both)
 
 
 def turn(z, num, den):
@@ -103,17 +103,28 @@
     return rows
 
 
-def block_work(load, pairs, taps, high, low, twist, out, acc, filt, left_hi, left_lo, mid, spec):
+def block_work(load, pairs, taps, weights, twist, out, acc, tapd, filt, left_hi, left_lo, mid, spec):
     streams = spec.shape[0]
-    ntaps, rows_frame = taps.shape[0], taps.shape[1]
-    radix = rows_frame // 2
+    ntaps, radix = taps.shape[0], taps.shape[1] // LANES
+    rows_frame = 2 * radix
+
+    @pl.when(pl.program_id(0) == 0)
+    def _():
+        acc[...] = jnp.zeros_like(acc)
+        for r in range(radix):
+            row = taps[:, r * LANES : (r + 1) * LANES]
+            for comp in range(2):
+                tapd[pl.ds(2 * r + comp, ntaps, stride=rows_frame), :] = row
 
     @pl.loop(0, streams)
     def _(s):
         @pl.loop(0, rows_frame // SUB)
         def _(c):
             rows = pl.ds(pl.multiple_of(c * SUB, SUB), SUB)
-            tap = [taps[t, rows, :] for t in range(ntaps)]
+            tap = [
+                tapd[pl.ds(pl.multiple_of(t * rows_frame + c * SUB, SUB), SUB), :]
+                for t in range(ntaps)
+            ]
             x = [load(s, i, rows).astype(jnp.float32) for i in range(SUB + ntaps - 1)]
             for f in range(SUB):
                 total = tap[0] * x[f + ntaps - 1]
@@ -140,7 +151,7 @@
     def _(s):
         at = pl.ds(pl.multiple_of(s * radix * SUB, radix * SUB), radix * SUB)
         hi, lo = left_hi[at, :], left_lo[at, :]
-        mid[at, :] = dot(hi, high[...]) + (dot(lo, high[...]) + dot(hi, low[...]))
+        mid[at, :] = dot(hi, weights[0]) + (dot(lo, weights[0]) + dot(hi, weights[1]))
 
     @pl.loop(0, streams)
     def _(s):
@@ -149,14 +160,14 @@
             at = pl.ds(pl.multiple_of(s * radix * SUB + b * SUB, SUB), SUB)
             re, im = mid[at, 0:LANES], mid[at, LANES : 2 * LANES]
             if b:
-                c, n = twist[0, b], twist[1, b]
+                c, n = twist[0, b : b + 1, :], twist[1, b : b + 1, :]
                 re, im = re * c + im * n, im * c - re * n
             items.append((re, im))
         for k, z in enumerate(dft(items)):
             spec[s, 0, k] = z[0]
             spec[s, 1, k] = z[1]
 
-    npairs = pairs.shape[0]
+    npairs = pairs.shape[1]
 
     @pl.loop(0, radix)
     def _(k):
@@ -165,7 +176,7 @@
             re, im = spec[s, 0, k], spec[s, 1, k]
             acc[s, :, cols] += re * re + im * im
         for p in range(npairs):
-            a, b = pairs[p, 0], pairs[p, 1]
+            a, b = pairs[0, p], pairs[1, p]
             lr, li, rr, ri = spec[a, 0, k], spec[a, 1, k], spec[b, 0, k], spec[b, 1, k]
             pr = lr * rr + li * ri
             pi = li * rr - lr * ri
@@ -180,12 +191,8 @@
         sums[i : i + 1, :] = jnp.sum(acc[i], axis=0, keepdims=True)
 
 
-def inner_kernel(pairs, pp, p, c, taps, high, low, twist, out, sums, acc, *scratch):
+def inner_kernel(pairs, pp, p, c, taps, weights, twist, out, sums, acc, *scratch):
     j = pl.program_id(0)
-
-    @pl.when(j == 0)
-    def _():
-        acc[...] = jnp.zeros_like(acc)
 
     def load(s, i, rows):
         if i < 7:
@@ -194,19 +201,15 @@
             return p[s, i - 7, rows, :]
         return c[s, i - 15, rows, :]
 
-    block_work(load, pairs, taps, high, low, twist, out, acc, *scratch)
+    block_work(load, pairs, taps, weights, twist, out, acc, *scratch)
 
     @pl.when(j == pl.num_programs(0) - 1)
     def _():
         finish(acc, sums)
 
 
-def edge_kernel(pairs, halo, c0, c, taps, high, low, twist, _, out, sums, acc, *scratch):
+def edge_kernel(pairs, halo, c0, c, taps, weights, twist, _, out, sums, acc, *scratch):
     j = pl.program_id(0)
-
-    @pl.when(j == 0)
-    def _():
-        acc[...] = jnp.zeros_like(acc)
 
     def load(s, i, rows):
         if i < 7:
@@ -215,31 +218,128 @@
             return jnp.where(j == 0, halo[s, i, rows, :], c0[s, i - 7, rows, :])
         return c[s, i - 15, rows, :]
 
-    block_work(load, pairs, taps, high, low, twist, out, acc, *scratch)
+    block_work(load, pairs, taps, weights, twist, out, acc, *scratch)
 
     @pl.when(j == pl.num_programs(0) - 1)
     def _():
         finish(acc, sums)
 
 
-def scale_kernel(frames_all, pairs, sums, prod, coherence, out):
-    npairs = pairs.shape[0]
-    streams = sums.shape[0] - 2 * npairs
-    for p in range(npairs):
-        a, b = pairs[p, 0], pairs[p, 1]
-        mean_a = sums[pl.ds(a, 1), :] / frames_all
-        mean_b = sums[pl.ds(b, 1), :] / frames_all
-        re = sums[streams + p : streams + p + 1, :] / frames_all
-        im = sums[streams + npairs + p : streams + npairs + p + 1, :] / frames_all
-        denom = (mean_a + 1e-06) * (mean_b + 1e-06)
-
-        @pl.when(pl.program_id(0) == 0)
-        def _():
-            coherence[p : p + 1, :] = (re * re + im * im) / denom
-
-        factor = 1.0 / jnp.sqrt(denom)
-        out[0, p] = prod[0, p] * factor
-        out[1, p] = prod[1, p] * factor
+def reduce_kernel(n, owners, frames_all, pairs, a, b, out, send, recv, part, got, s1, r1, s2, r2):
+    me = lax.axis_index("tm")
+    radix = send.shape[0]
+    per = radix // owners
+    npairs = pairs.shape[1]
+    streams = send.shape[1] - 2 * npairs
+    everyone = owners == n
+
+    def peer(d):
+        return lax.rem(me + d, n)
+
+    def source(d):
+        return lax.rem(me + n - d, n)
+
+    def guarded(cond, do):
+        if everyone:
+            do()
+        else:
+            pl.when(cond)(do)
+
+    def scatter(d):
+        return pltpu.make_async_remote_copy(
+            src_ref=send.at[pl.ds(peer(d) * per, per)],
+            dst_ref=recv.at[d],
+            send_sem=s1.at[d],
+            recv_sem=r1.at[d],
+            device_id={"tm": peer(d)},
+            device_id_type=pl.DeviceIdType.MESH,
+        )
+
+    def spread(d, owner):
+        return pltpu.make_async_remote_copy(
+            src_ref=part,
+            dst_ref=got.at[pl.ds(owner * per, per)],
+            send_sem=s2.at[d],
+            recv_sem=r2.at[d],
+            device_id={"tm": peer(d)},
+            device_id_type=pl.DeviceIdType.MESH,
+        )
+
+    barrier = pltpu.get_barrier_semaphore()
+
+    @pl.loop(1, n)
+    def _(d):
+        pl.semaphore_signal(
+            barrier, inc=1, device_id={"tm": peer(d)}, device_id_type=pl.DeviceIdType.MESH
+        )
+
+    for k in range(radix):
+        cols = slice(k * LANES, (k + 1) * LANES)
+        send[k] = a[:, cols] + b[:, cols]
+    pl.semaphore_wait(barrier, n - 1)
+
+    @pl.loop(1, n)
+    def _(d):
+        guarded(peer(d) < owners, lambda: scatter(d).start())
+
+    def own():
+        @pl.loop(1, n)
+        def _(d):
+            scatter(d).wait_recv()
+
+        def more(d, total):
+            return total + recv[d]
+
+        total = lax.fori_loop(1, n, more, send[pl.ds(me * per, per)]) / frames_all
+        auto = [total[:, s : s + 1, :] + 1e-06 for s in range(streams)]
+
+        def pick(s):
+            value = auto[0]
+            for i in range(1, streams):
+                value = jnp.where(s == i, auto[i], value)
+            return value
+
+        for p in range(npairs):
+            re = total[:, streams + p : streams + p + 1, :]
+            im = total[:, streams + npairs + p : streams + npairs + p + 1, :]
+            denom = pick(pairs[0, p]) * pick(pairs[1, p])
+            part[:, p : p + 1, :] = 1.0 / jnp.sqrt(denom)
+            part[:, npairs + p : npairs + p + 1, :] = (re * re + im * im) / denom
+
+        @pl.loop(1, n)
+        def _(d):
+            spread(d, me).start()
+
+        got[pl.ds(me * per, per)] = part[...]
+
+    guarded(me < owners, own)
+
+    @pl.loop(1, n)
+    def _(d):
+        guarded(source(d) < owners, lambda: spread(d, source(d)).wait_recv())
+
+    out[...] = got[...]
+
+    @pl.loop(1, n)
+    def _(d):
+        guarded(peer(d) < owners, lambda: scatter(d).wait_send())
+        guarded(me < owners, lambda: spread(d, me).wait_send())
+
+
+def scale_kernel(table, prod, coherence, out):
+    npairs = prod.shape[1]
+
+    @pl.when(pl.program_id(0) == 0)
+    def _():
+        for k in range(table.shape[0]):
+            coherence[:, k * LANES : (k + 1) * LANES] = table[k, npairs:, :]
+
+    for k in range(table.shape[0]):
+        cols = slice(k * LANES, (k + 1) * LANES)
+        for p in range(npairs):
+            factor = table[k, p : p + 1, :]
+            out[0, p, :, cols] = prod[0, p, :, cols] * factor
+            out[1, p, :, cols] = prod[1, p, :, cols] * factor
 
 
 def on_device(volts, taps, pairs):
@@ -256,13 +356,14 @@
     view = view.reshape(streams, frames, rows_frame, LANES)
     size = lax.axis_size("tm")
     halo = lax.ppermute(view[:, frames - edge :], "tm", [(i, i + 1) for i in range(size - 1)])
-    taps2 = jnp.repeat(taps.reshape(ntaps, radix, LANES), comps, axis=1)
-    high, low = matrices(channels)
+    pairs = pairs.T
+    weights = matrices(channels)
     twist = twiddles(channels)
 
     rows = streams * radix * SUB
     scratch = [
         pltpu.VMEM((nsums, SUB, channels), jnp.float32),
+        pltpu.VMEM((ntaps * rows_frame, LANES), jnp.float32),
         pltpu.VMEM((streams, SUB * rows_frame, LANES), jnp.float32),
         pltpu.VMEM((rows, 2 * LANES), jnp.bfloat16),
         pltpu.VMEM((rows, 2 * LANES), jnp.bfloat16),
@@ -275,10 +376,9 @@
         return pl.BlockSpec(dims, lambda j: (0,) * len(dims))
 
     tables = [
-        whole(ntaps, rows_frame, LANES),
-        whole(2 * LANES, 2 * LANES),
-        whole(2 * LANES, 2 * LANES),
-        whole(2, radix, SUB, LANES),
+        whole(ntaps, channels),
+        whole(2, 2 * LANES, 2 * LANES),
+        whole(2, radix, LANES),
     ]
     frame_dims = (streams, SUB, rows_frame, LANES)
     prod_dims = (2, npairs, SUB, channels)
@@ -307,7 +407,7 @@
         compiler_params=params(),
         cost_estimate=cost(blocks - first),
         name="inner",
-    )(pairs, view, view, view, taps2, high, low, twist)
+    )(pairs, view, view, view, taps, weights, twist)
 
     prod, sums_edge = pl.pallas_call(
         edge_kernel,
@@ -322,22 +422,47 @@
         ],
         out_shape=[prod_type, sums_type],
         scratch_shapes=scratch,
-        input_output_aliases={8: 0},
+        input_output_aliases={7: 0},
         compiler_params=params(),
         cost_estimate=cost(first),
         name="edge",
-    )(pairs, halo, view, view, taps2, high, low, twist, prod)
-
-    sums = lax.psum(sums_inner + sums_edge, "tm")
+    )(pairs, halo, view, view, taps, weights, twist, prod)
+
+    owners = math.gcd(size, radix)
+    per = radix // owners
+    vmem = pl.BlockSpec(memory_space=pltpu.VMEM)
+    dma = pltpu.SemaphoreType.DMA((size,))
+    table = pl.pallas_call(
+        functools.partial(reduce_kernel, size, owners, frames * size),
+        in_specs=[smem, vmem, vmem],
+        out_specs=vmem,
+        out_shape=jax.ShapeDtypeStruct((radix, 2 * npairs, LANES), jnp.float32),
+        scratch_shapes=[
+            pltpu.VMEM((radix, nsums, LANES), jnp.float32),
+            pltpu.VMEM((size, per, nsums, LANES), jnp.float32),
+            pltpu.VMEM((per, 2 * npairs, LANES), jnp.float32),
+            pltpu.VMEM((radix, 2 * npairs, LANES), jnp.float32),
+            dma,
+            dma,
+            dma,
+            dma,
+        ],
+        compiler_params=pltpu.CompilerParams(collective_id=0, has_side_effects=True),
+        name="reduce",
+    )(pairs, sums_inner, sums_edge)
+
     coherence, normalized = pl.pallas_call(
-        functools.partial(scale_kernel, frames * size),
+        scale_kernel,
         grid=(blocks,),
-        in_specs=[smem, whole(nsums, channels), pl.BlockSpec(prod_dims, lambda j: (0, 0, j, 0))],
+        in_specs=[
+            whole(radix, 2 * npairs, LANES),
+            pl.BlockSpec(prod_dims, lambda j: (0, 0, j, 0)),
+        ],
         out_specs=[whole(npairs, channels), pl.BlockSpec(prod_dims, lambda j: (0, 0, j, 0))],
         out_shape=[jax.ShapeDtypeStruct((npairs, channels), jnp.float32), prod_type],
         compiler_params=params(),
         name="scale",
-    )(pairs, sums, prod)
+    )(table, prod)
     return (coherence, normalized)
 
 

time: 171 us -> 81.6 us (0.48)
  waiting for transfers between devices: 92.4 us -> 0.01 us
  Pallas kernels: 51.8 us -> 71.2 us
  between operations: 14.1 us -> 0.68 us
  local copies, waits for them, and re-layouts: 8.54 us -> 6.7 us
    psum x1 -> x0, waiting for transfers between devices: 92.3 us -> none  [on_device(): sums = lax.psum(sums_inner + sums_edge, 'tm')]
    pallas_call x1 -> x2, Pallas kernels: 7.21 us -> 26 us  [the longest x1 19.1 us: on_device(): pl.pallas_call(functools.partial(reduce_kernel, size, owners, frames * si...]
    unnamed x8 -> x14, local copies, waits for them, and re-layouts: 4.52 us -> 4.93 us
  transfers between devices with their start and end apart: 2 -> 1, of which waited for: 1 -> 0; matrix products, arithmetic and copies ran while one was open for 2% -> 0% of each run, Pallas kernels for 17% -> 36%
where the time goes in v1:
time: 81.6 us; the launch traced here: 81.1 us
  Pallas kernels  71.2 us (87%)
  local copies, waits for them, and re-layouts  6.7 us (8%)
  starting transfers between devices  2.52 us (3%)
    pallas_call x1, Pallas kernels, on_device(): pl.pallas_call(inner_kernel, grid=(blocks - first,), in_specs=[smem] + [p...  28.9 us
    pallas_call x1, Pallas kernels, on_device(): pl.pallas_call(functools.partial(reduce_kernel, size, owners, frames * si...  19.1 us
    pallas_call x1, Pallas kernels, on_device(): pl.pallas_call(edge_kernel, grid=(first,), in_specs=[smem, whole(streams,...  16.4 us
    pallas_call x1, Pallas kernels, on_device(): pl.pallas_call(scale_kernel, grid=(blocks,), in_specs=[whole(radix, 2 * n...  6.92 us
    unnamed x14, local copies, waits for them, and re-layouts  4.93 us
    ppermute x1, starting transfers between devices, on_device(): lax.ppermute(view[:, frames - edge:], 'tm', [(i, i + 1) for i in range(si...  2.52 us
    slice x1, local copies, waits for them, and re-layouts, on_device(): view[:, frames - edge:]  1.77 us
  transfers between devices with their start and end apart: 1, of which 0 were waited for; matrix products, arithmetic and copies ran while one was open for 0% of the time, Pallas kernels for 36%

profile of v1, /device:TPU:0, one launch (start us, length us, event | category | flops | bytes accessed | tf_op | source)
XLA Modules:
  0.0 81.1 jit_solution(7460144459298030389)
XLA Ops:
  0.6 1.8 %slice.4 = s32[4,15,64,128]{3,2,1,0:T(8,128)S(1)} slice(s32[4,48,64,128]{3,2,1,0:T(8,128)} %bitcast.9), slice={[0:4], [33:48], [0:64], [0:128]} | slice | bytes 3932160 | tf_op jit(solution)/shard_map/slice | solution.py:358
  2.4 2.5 %collective-permute-start = (s32[4,15,64,128]{3,2,1,0:T(8,128)S(1)}, s32[4,15,64,128]{3,2,1,0:T(8,128)S(1)}, u32[]{:S(2)}, u32[]{:S(2)}) collective-permute-start(s32[4,15,64,128]{3,2,1,0:T(8,128)S(1)} %slice.4), channel_id=1, source_target_pairs={{0,1},{1,2},{2,3},{3,4},{4,5},{5,6},{6,7},{7,8},{8,9},{9,10},{10,1... | collective-permute-start | bytes 5898248 | tf_op jit(solution)/shard_map/ppermute | solution.py:358
  4.9 0.0 copy-start
  4.9 0.9 %copy-done = f32[16,4096]{1,0:T(8,128)S(1)} copy-done((f32[16,4096]{1,0:T(8,128)S(1)}, f32[16,4096]{1,0:T(8,128)}, u32[]{:S(2)}) %copy-start) | copy-done | bytes 262168
  5.9 0.0 copy-start.1
  5.9 0.9 %copy-done.1 = bf16[2,256,256]{2,1,0:T(8,128)(2,1)S(1)} copy-done((bf16[2,256,256]{2,1,0:T(8,128)(2,1)S(1)}, bf16[2,256,256]{2,1,0:T(8,128)(2,1)}, u32[]{:S(2)}) %copy-start.1) | copy-done | bytes 262168
  6.8 0.0 copy-start.5
  6.8 0.8 copy-done.5
  7.6 0.0 copy-start.6
  7.6 0.7 copy-done.6
  8.3 28.9 %inner.1 = (f32[2,4,48,4096]{3,2,1,0:T(8,128)}, f32[12,4096]{1,0:T(8,128)S(1)}) custom-call(s32[2,4]{1,0:T(2,128)S(1)} %bitcast.7, s32[4,48,64,128]{3,2,1,0:T(8,128)} %bitcast.10, s32[4,48,64,128]{3,2,1,0:T(8,128)} %bitcast.11, s32[4,48,64,128]{3,2,1,0:T(8,128)} %bitcast.12, f32[16,4096]{1,0:T(8,128)S(1)} %copy-done, bf16[2,256,256]{2,1,0:T(8,128)(2,1)S(1)} %copy-done.1, ...), custom_call_target="tpu_custom_call" | custom-call | flops 2000000000 | bytes 16000000 | tf_op jit(solution)/shard_map/inner/pallas_call | solution.py:395
  37.2 0.0 copy-start.3
  37.2 0.0 collective-permute-done.halo
  37.2 16.4 %edge.1 = (f32[2,4,48,4096]{3,2,1,0:T(8,128)}, f32[12,4096]{1,0:T(8,128)S(1)}) custom-call(s32[2,4]{1,0:T(2,128)S(1)} %bitcast.8, s32[4,15,64,128]{3,2,1,0:T(8,128)S(1)} %collective-permute-done.halo, s32[4,48,64,128]{3,2,1,0:T(8,128)} %bitcast.13, s32[4,48,64,128]{3,2,1,0:T(8,128)} %bitcast.14, ...), custom_call_target="tpu_custom_call", output_to_operand_aliasing={{0}: (7, {})} | custom-call | flops 1000000000 | bytes 8000000 | tf_op jit(solution)/shard_map/edge/pallas_call | solution.py:412
  53.5 0.0 copy-done.3
  53.5 0.0 copy-start.4
  53.5 0.7 copy-done.4
  54.2 19.1 %reduce.1.table = f32[32,8,128]{2,1,0:T(8,128)} custom-call(s32[2,4]{1,0:T(2,128)} %bitcast.6, f32[12,4096]{1,0:T(8,128)} %copy-done.3, f32[12,4096]{1,0:T(8,128)} %copy-done.4), custom_call_target="tpu_custom_call" | custom-call | tf_op jit(solution)/shard_map/reduce/pallas_call | solution.py:435
  73.3 0.0 copy-start.2
  73.3 0.9 %copy-done.2 = f32[32,8,128]{2,1,0:T(8,128)S(1)} copy-done((f32[32,8,128]{2,1,0:T(8,128)S(1)}, f32[32,8,128]{2,1,0:T(8,128)}, u32[]{:S(2)}) %copy-start.2) | copy-done | bytes 131096
  74.2 6.9 %scale.1 = (f32[4,4096]{1,0:T(4,128)}, f32[2,4,48,4096]{3,2,1,0:T(8,128)}) custom-call(f32[32,8,128]{2,1,0:T(8,128)S(1)} %copy-done.2, f32[2,4,48,4096]{3,2,1,0:T(8,128)} %get-tuple-element.9.prod), custom_call_target="tpu_custom_call" | custom-call | tf_op jit(solution)/shard_map/scale/pallas_call | solution.py:454
Async XLA Ops:
  2.4 34.8 %collective-permute-start = (s32[4,15,64,128]{3,2,1,0:T(8,128)S(1)}, s32[4,15,64,128]{3,2,1,0:T(8,128)S(1)}, u32[]{:S(2)}, u32[]{:S(2)}) collective-permute-start(s32[4,15,64,128]{3,2,1,0:T(8,128)S(1)} %slice.4), channel_id=1, source_target_pairs={{0,1},{1,2},{2,3},{3,4},{4,5},{5,6},{6,7},{7,8},{8,9},{9,10},{10,1... | collective-permute-start | bytes 5898248 | tf_op jit(solution)/shard_map/ppermute | solution.py:358
  4.9 1.0 %copy-start = (f32[16,4096]{1,0:T(8,128)S(1)}, f32[16,4096]{1,0:T(8,128)}, u32[]{:S(2)}) copy-start(f32[16,4096]{1,0:T(8,128)} %taps.3) | copy-start | bytes 786436
  5.9 0.9 %copy-start.1 = (bf16[2,256,256]{2,1,0:T(8,128)(2,1)S(1)}, bf16[2,256,256]{2,1,0:T(8,128)(2,1)}, u32[]{:S(2)}) copy-start(bf16[2,256,256]{2,1,0:T(8,128)(2,1)} %constant.4.clone.weights) | copy-start | bytes 786436
  6.8 0.8 copy-start.5
  7.6 0.7 copy-start.6
  37.2 16.4 %copy-start.3 = (f32[12,4096]{1,0:T(8,128)}, f32[12,4096]{1,0:T(8,128)S(1)}, u32[]{:S(2)}) copy-start(f32[12,4096]{1,0:T(8,128)S(1)} %get-tuple-element.6.a) | copy-start | bytes 589828
  53.5 0.7 copy-start.4
  73.3 0.9 %copy-start.2 = (f32[32,8,128]{2,1,0:T(8,128)S(1)}, f32[32,8,128]{2,1,0:T(8,128)}, u32[]{:S(2)}) copy-start(f32[32,8,128]{2,1,0:T(8,128)} %reduce.1.table) | copy-start | bytes 393220

commit v2 on v1

--- a/solution.py
+++ b/solution.py
@@ -88,25 +88,11 @@
     return out
 
 
-def swap_lanes(rows):
-    rows = list(rows)
-    lane = lax.broadcasted_iota(jnp.int32, (SUB, LANES), 1)
-    step = 1
-    while step < len(rows):
-        low = (lane & step) == 0
-        for i in range(len(rows)):
-            if i & step == 0:
-                a, b = rows[i], rows[i + step]
-                rows[i] = jnp.where(low, a, pltpu.roll(b, step, 1))
-                rows[i + step] = jnp.where(low, pltpu.roll(a, LANES - step, 1), b)
-        step *= 2
-    return rows
-
-
 def block_work(load, pairs, taps, weights, twist, out, acc, tapd, filt, left_hi, left_lo, mid, spec):
     streams = spec.shape[0]
     ntaps, radix = taps.shape[0], taps.shape[1] // LANES
     rows_frame = 2 * radix
+    pitch = rows_frame + 1
 
     @pl.when(pl.program_id(0) == 0)
     def _():
@@ -114,36 +100,77 @@
         for r in range(radix):
             row = taps[:, r * LANES : (r + 1) * LANES]
             for comp in range(2):
-                tapd[pl.ds(2 * r + comp, ntaps, stride=rows_frame), :] = row
-
-    @pl.loop(0, streams)
+                tapd[pl.ds(2 * r + comp, ntaps, stride=pitch), :] = row
+
+    def fir(s, c):
+        rows = pl.ds(pl.multiple_of(c * SUB, SUB), SUB)
+        tap = [
+            tapd[pl.ds(t * pitch + c * SUB, SUB), :]
+            for t in range(ntaps)
+        ]
+        x = [load(s, i, rows).astype(jnp.float32) for i in range(SUB + ntaps - 1)]
+        for f in range(SUB):
+            total = tap[0] * x[f + ntaps - 1]
+            for t in range(1, ntaps):
+                total = total + tap[t] * x[f + ntaps - 1 - t]
+            filt[s, pl.ds(f * pitch + c * SUB, SUB), :] = total
+
+    def low_bit(step):
+        return (lax.broadcasted_iota(jnp.int32, (SUB, LANES), 1) & step) == 0
+
+    def exchange(a, b, step):
+        low = low_bit(step)
+        return (
+            jnp.where(low, a, pltpu.roll(b, step, 1)),
+            jnp.where(low, pltpu.roll(a, LANES - step, 1), b),
+        )
+
+    def swap(stream):
+        sets = [(stream, comp) for comp in range(2)]
+        for s, comp in sets:
+            for g in range(0, radix, 4):
+                v = [
+                    filt[s, pl.ds(2 * r + comp, SUB, stride=pitch), :]
+                    for r in range(g, g + 4)
+                ]
+                v[0], v[1] = exchange(v[0], v[1], 1)
+                v[2], v[3] = exchange(v[2], v[3], 1)
+                v[0], v[2] = exchange(v[0], v[2], 2)
+                v[1], v[3] = exchange(v[1], v[3], 2)
+                for i in range(4):
+                    spec[s, comp, g + i] = v[i]
+        for s, comp in sets:
+            for g in [16 * h + i for h in range(radix // 16) for i in range(4)]:
+                v = [spec[s, comp, g + 4 * i] for i in range(4)]
+                v[0], v[1] = exchange(v[0], v[1], 4)
+                v[2], v[3] = exchange(v[2], v[3], 4)
+                v[0], v[2] = exchange(v[0], v[2], 8)
+                v[1], v[3] = exchange(v[1], v[3], 8)
+                for i in range(4):
+                    spec[s, comp, g + 4 * i] = v[i]
+        for s, comp in sets:
+            for b in range(0, radix // 2, 2):
+                v = [exchange(spec[s, comp, b + i], spec[s, comp, b + i + 16], 16) for i in range(2)]
+                for half in range(2):
+                    both = jnp.concatenate([v[0][half], v[1][half]], axis=0)
+                    hi = both.astype(jnp.bfloat16)
+                    lo = (both - hi.astype(jnp.float32)).astype(jnp.bfloat16)
+                    at = pl.multiple_of(s * radix * SUB + (b + 16 * half) * SUB, 2 * SUB)
+                    where = (pl.ds(at, 2 * SUB), pl.ds(comp * LANES, LANES))
+                    left_hi[where] = hi
+                    left_lo[where] = lo
+
+    @pl.loop(0, rows_frame // SUB)
+    def _(c):
+        fir(0, c)
+
+    @pl.loop(0, streams - 1)
     def _(s):
-        @pl.loop(0, rows_frame // SUB)
-        def _(c):
-            rows = pl.ds(pl.multiple_of(c * SUB, SUB), SUB)
-            tap = [
-                tapd[pl.ds(pl.multiple_of(t * rows_frame + c * SUB, SUB), SUB), :]
-                for t in range(ntaps)
-            ]
-            x = [load(s, i, rows).astype(jnp.float32) for i in range(SUB + ntaps - 1)]
-            for f in range(SUB):
-                total = tap[0] * x[f + ntaps - 1]
-                for t in range(1, ntaps):
-                    total = total + tap[t] * x[f + ntaps - 1 - t]
-                at = pl.multiple_of(f * rows_frame + c * SUB, SUB)
-                filt[s, pl.ds(at, SUB), :] = total
-
-        for comp in range(2):
-            rows = [filt[s, pl.ds(2 * r + comp, SUB, stride=rows_frame), :] for r in range(radix)]
-            rows = swap_lanes(rows)
-            for b in range(0, radix, 2):
-                both = jnp.concatenate([rows[b], rows[b + 1]], axis=0)
-                hi = both.astype(jnp.bfloat16)
-                lo = (both - hi.astype(jnp.float32)).astype(jnp.bfloat16)
-                at = pl.multiple_of(s * radix * SUB + b * SUB, 2 * SUB)
-                where = (pl.ds(at, 2 * SUB), pl.ds(comp * LANES, LANES))
-                left_hi[where] = hi
-                left_lo[where] = lo
+        swap(s)
+        for c in range(rows_frame // SUB):
+            fir(s + 1, c)
+
+    swap(streams - 1)
 
     dot = functools.partial(jnp.dot, preferred_element_type=jnp.float32)
 
@@ -363,8 +390,8 @@
     rows = streams * radix * SUB
     scratch = [
         pltpu.VMEM((nsums, SUB, channels), jnp.float32),
-        pltpu.VMEM((ntaps * rows_frame, LANES), jnp.float32),
-        pltpu.VMEM((streams, SUB * rows_frame, LANES), jnp.float32),
+        pltpu.VMEM((ntaps * (rows_frame + 1), LANES), jnp.float32),
+        pltpu.VMEM((streams, SUB * (rows_frame + 1), LANES), jnp.float32),
         pltpu.VMEM((rows, 2 * LANES), jnp.bfloat16),
         pltpu.VMEM((rows, 2 * LANES), jnp.bfloat16),
         pltpu.VMEM((rows, 2 * LANES), jnp.float32),
@@ -387,7 +414,7 @@
     first = 2
 
     def params():
-        return pltpu.CompilerParams(vmem_limit_bytes=48 * 1024 * 1024)
+        return pltpu.CompilerParams(vmem_limit_bytes=63 * 1024 * 1024)
 
     def cost(n):
         return pl.CostEstimate(flops=n * 500_000_000, bytes_accessed=n * 4_000_000, transcendentals=0)

time: 81.6 us -> 88.5 us (1.085)
  Pallas kernels: 71.2 us -> 80.8 us
  local copies, waits for them, and re-layouts: 6.7 us -> 3.05 us
  starting transfers between devices: 2.52 us -> 3.69 us
    pallas_call x1, Pallas kernels: 28.9 us -> 35.8 us  [on_device(): pl.pallas_call(inner_kernel, grid=(blocks - first,), in_specs=[smem] + [p...]
    unnamed x14 -> x0, local copies, waits for them, and re-layouts: 4.93 us -> none
    pallas_call x1, Pallas kernels: 16.4 us -> 20.2 us  [on_device(): pl.pallas_call(edge_kernel, grid=(first,), in_specs=[smem, whole(streams,...]
    slice x1, local copies, waits for them, and re-layouts: 1.77 us -> 3.05 us  [on_device(): view[:, frames - edge:]]
    ppermute x1, starting transfers between devices: 2.52 us -> 3.69 us  [on_device(): lax.ppermute(view[:, frames - edge:], 'tm', [(i, i + 1) for i in range(si...]
    pallas_call x1, Pallas kernels: 19.1 us -> 17.9 us  [on_device(): pl.pallas_call(functools.partial(reduce_kernel, size, owners, frames * si...]
  transfers between devices with their start and end apart: 1 -> 1, of which waited for: 0 -> 0; matrix products, arithmetic and copies ran while one was open for 0% -> 0% of each run, Pallas kernels for 36% -> 41%
where the time goes in v2:
time: 88.5 us; the launch traced here: 88.2 us
  Pallas kernels  80.8 us (91%)
  starting transfers between devices  3.69 us (4%)
  local copies, waits for them, and re-layouts  3.05 us (3%)
    pallas_call x1, Pallas kernels, on_device(): pl.pallas_call(inner_kernel, grid=(blocks - first,), in_specs=[smem] + [p...  35.8 us
    pallas_call x1, Pallas kernels, on_device(): pl.pallas_call(edge_kernel, grid=(first,), in_specs=[smem, whole(streams,...  20.2 us
    pallas_call x1, Pallas kernels, on_device(): pl.pallas_call(functools.partial(reduce_kernel, size, owners, frames * si...  17.9 us
    pallas_call x1, Pallas kernels, on_device(): pl.pallas_call(scale_kernel, grid=(blocks,), in_specs=[whole(radix, 2 * n...  6.95 us
    ppermute x1, starting transfers between devices, on_device(): lax.ppermute(view[:, frames - edge:], 'tm', [(i, i + 1) for i in range(si...  3.69 us
    slice x1, local copies, waits for them, and re-layouts, on_device(): view[:, frames - edge:]  3.05 us
  transfers between devices with their start and end apart: 1, of which 0 were waited for; matrix products, arithmetic and copies ran while one was open for 0% of the time, Pallas kernels for 41%

profile of v2, /device:TPU:0, one launch (start us, length us, event | category | flops | bytes accessed | tf_op | source)
XLA Modules:
  0.0 88.2 jit_solution(17329293469199106828)
XLA Ops:
  0.6 3.1 %slice.4 = s32[4,15,64,128]{3,2,1,0:T(8,128)} slice(s32[4,48,64,128]{3,2,1,0:T(8,128)} %bitcast.6), slice={[0:4], [33:48], [0:64], [0:128]} | slice | bytes 3932160 | tf_op jit(solution)/shard_map/slice | solution.py:385
  3.7 3.7 %collective-permute-start = (s32[4,15,64,128]{3,2,1,0:T(8,128)}, s32[4,15,64,128]{3,2,1,0:T(8,128)}, u32[]{:S(2)}, u32[]{:S(2)}) collective-permute-start(s32[4,15,64,128]{3,2,1,0:T(8,128)} %slice.4), channel_id=1, source_target_pairs={{0,1},{1,2},{2,3},{3,4},{4,5},{5,6},{6,7},{7,8},{8,9},{9,10},{10,1... | collective-permute-start | bytes 5898248 | tf_op jit(solution)/shard_map/ppermute | solution.py:385
  7.4 35.8 %inner.1 = (f32[2,4,48,4096]{3,2,1,0:T(8,128)}, f32[12,4096]{1,0:T(8,128)}) custom-call(s32[2,4]{1,0:T(2,128)} %bitcast.12, s32[4,48,64,128]{3,2,1,0:T(8,128)} %bitcast.7, s32[4,48,64,128]{3,2,1,0:T(8,128)} %bitcast.8, s32[4,48,64,128]{3,2,1,0:T(8,128)} %bitcast.9, f32[16,4096]{1,0:T(8,128)} %taps.3, bf16[2,256,256]{2,1,0:T(8,128)(2,1)} %constant.4.clone.weights, ...), custom_call_target="tpu_custom_call" | custom-call | flops 2000000000 | bytes 16000000 | tf_op jit(solution)/shard_map/inner/pallas_call | solution.py:422
  43.1 0.0 collective-permute-done.halo
  43.1 20.2 %edge.1 = (f32[2,4,48,4096]{3,2,1,0:T(8,128)}, f32[12,4096]{1,0:T(8,128)}) custom-call(s32[2,4]{1,0:T(2,128)} %bitcast.13, s32[4,15,64,128]{3,2,1,0:T(8,128)} %collective-permute-done.halo, s32[4,48,64,128]{3,2,1,0:T(8,128)} %bitcast.10, s32[4,48,64,128]{3,2,1,0:T(8,128)} %bitcast.11, f32[16,4096]{1,0:T(8,128)} %taps.3, ...), custom_call_target="tpu_custom_call", output_to_operand_aliasing={{0}: (7, {})} | custom-call | flops 1000000000 | bytes 8000000 | tf_op jit(solution)/shard_map/edge/pallas_call | solution.py:439
  63.3 17.9 %reduce.1.table = f32[32,8,128]{2,1,0:T(8,128)} custom-call(s32[2,4]{1,0:T(2,128)} %bitcast.14, f32[12,4096]{1,0:T(8,128)} %get-tuple-element.6.a, f32[12,4096]{1,0:T(8,128)} %get-tuple-element.8.b), custom_call_target="tpu_custom_call" | custom-call | tf_op jit(solution)/shard_map/reduce/pallas_call | solution.py:462
  81.2 7.0 %scale.1 = (f32[4,4096]{1,0:T(4,128)}, f32[2,4,48,4096]{3,2,1,0:T(8,128)}) custom-call(f32[32,8,128]{2,1,0:T(8,128)} %reduce.1.table, f32[2,4,48,4096]{3,2,1,0:T(8,128)} %get-tuple-element.9.prod), custom_call_target="tpu_custom_call" | custom-call | tf_op jit(solution)/shard_map/scale/pallas_call | solution.py:481
Async XLA Ops:
  3.7 39.4 %collective-permute-start = (s32[4,15,64,128]{3,2,1,0:T(8,128)}, s32[4,15,64,128]{3,2,1,0:T(8,128)}, u32[]{:S(2)}, u32[]{:S(2)}) collective-permute-start(s32[4,15,64,128]{3,2,1,0:T(8,128)} %slice.4), channel_id=1, source_target_pairs={{0,1},{1,2},{2,3},{3,4},{4,5},{5,6},{6,7},{7,8},{8,9},{9,10},{10,1... | collective-permute-start | bytes 5898248 | tf_op jit(solution)/shard_map/ppermute | solution.py:385
